TPU v7x, 32 devices: a whole 2x2x4 slice. The times are simulated.
32 devices in a mesh: groups: 2 (over x), row: 8 (over z, y), head: 2 (over core).
Axes of the slice: x: 2, y: 2, z: 4, core: 2. Of those that a mesh axis runs over, the one named last changes fastest.
Arguments:
- hidden: bfloat16 [48, 4096], P('groups'), parts along dimension 0, may hold values from -6 to 6
- norm_gain: float32 [4096], replicated, may hold values from 0.1 to 1.9
- w_query: bfloat16 [8, 256, 4096], P('head', 'row'), may hold values from -0.09375 to 0.09375
- w_key: bfloat16 [8, 256, 4096], P('head', 'row'), may hold values from -0.09375 to 0.09375
- w_value: bfloat16 [8, 512, 4096], P('head', 'row'), may hold values from -0.09375 to 0.09375
- w_outgate: bfloat16 [8, 512, 4096], P('head', 'row'), may hold values from -0.09375 to 0.09375
- w_out: bfloat16 [8, 512, 4096], P('head', 'row'), may hold values from -0.125 to 0.125
- w_gates: bfloat16 [2, 8, 4096], P(None, 'head'), may hold values from -0.09375 to 0.09375
- gate_bias: float32 [2, 8], P(None, 'head'), may hold values from -2 to 4
- headnorm_gain: float32 [8, 512], P('head', 'row'), may hold values from 0.1 to 1.9
- final_gain: float32 [4096], replicated, may hold values from 0.1 to 1.9
- w_vocab: bfloat16 [25152, 4096], P(('row', 'head')), may hold values from -39.0625 to 39.0625
- memory: float32 [48, 8, 256, 512], P('groups', 'head', 'row'), parts along dimension 0, may hold values from -6 to 6
- normalizer: float32 [48, 8, 256], P('groups', 'head', 'row'), parts along dimension 0, may hold values from -6 to 6
- stabilizer: float32 [48, 8], P('groups', 'head'), parts along dimension 0, may hold values from -2 to 2
- targets: int32 [48], P('groups'), parts along dimension 0, may hold values from 0 to 25151
Outputs:
- memory_out: float32 [48, 8, 256, 512], P('groups', 'head', 'row'), parts along dimension 0
- normalizer_out: float32 [48, 8, 256], P('groups', 'head', 'row'), parts along dimension 0
- stabilizer_out: float32 [48, 8], P('groups', 'head'), parts along dimension 0
- hidden_out: bfloat16 [48, 4096], P('groups', ('row', 'head')), parts along dimension 0
- log_prob: float32 [48], P('groups'), parts along dimension 0
There are 2 independent parts, one for each index of `groups`. A program takes and returns all parts, laid end to end along the dimension named above; an argument that names none is the same for every part. Nothing has to cross between parts.
All inputs are finite; a program needn't handle non-finite values.
Results may differ from a plain program's by a relative error of at most 0.0035.
The roundings to bfloat16 on the way count: a program that leaves them out, or rounds other values in their place, can miss the bound.
Values may be sent and summed in bfloat16 or wider, within the bound.
A program may use at most 64 MiB of HBM per device.

v0:
```python
import math
import jax
import jax.numpy as jnp
from jax import lax
from jax.sharding import PartitionSpec as P

QK_DIM = 256
epsilon = 1e-06


def joined_2(value, axis, join):
    pieces = jax.tree.map(lambda part: lax.all_gather(part, axis), value)
    head = jax.tree.map(lambda part: part[0], pieces)
    tail = jax.tree.map(lambda part: part[1:], pieces)
    total, _ = lax.scan(lambda total, share: (join(total, share), None), head, tail)
    return total


def rms_round(stream, gain):
    scale = lax.rsqrt(jnp.mean(stream * stream, axis=-1, keepdims=True) + epsilon)
    return (stream * scale * gain).astype(jnp.bfloat16)


def per_device(
    hidden,
    norm_gain,
    w_query,
    w_key,
    w_value,
    w_outgate,
    w_out,
    w_gates,
    gate_bias,
    headnorm_gain,
    final_gain,
    w_vocab,
    memory,
    normalizer,
    stabilizer,
    targets,
):
    value_rows = w_value.shape[1]
    stream = hidden.astype(jnp.float32)
    normed_in = rms_round(stream, norm_gain)

    def project(weights):
        return jnp.einsum("sd,hjd->shj", normed_in, weights, preferred_element_type=jnp.float32)

    queries = project(w_query) / math.sqrt(QK_DIM)
    key_part = project(w_key)
    value_part = project(w_value).astype(jnp.bfloat16)
    outgate_pre = project(w_outgate)
    gate_pre = (
        jnp.einsum("sd,ghd->gsh", normed_in, w_gates, preferred_element_type=jnp.float32)
        + gate_bias[:, None, :]
    )
    log_forget = jax.nn.log_sigmoid(gate_pre[1])
    stabilizer_out = jnp.maximum(log_forget + stabilizer, gate_pre[0])
    decay_rate = jnp.exp(log_forget + stabilizer - stabilizer_out)
    inflow = jnp.exp(gate_pre[0] - stabilizer_out)
    scaled_key = inflow[:, :, None] * key_part
    memory_out = (
        decay_rate[:, :, None, None] * memory
        + scaled_key[:, :, :, None]
        * lax.all_gather(value_part, "row", axis=2, tiled=True).astype(jnp.float32)[:, :, None, :]
    )
    normalizer_out = decay_rate[:, :, None] * normalizer + scaled_key
    partial_readout = jnp.einsum(
        "shj,shje->she", queries, memory_out, precision=lax.Precision.HIGHEST
    )
    readout = lax.psum(partial_readout, "row")
    average = jnp.mean(readout, axis=-1)
    centered_full = readout - average[:, :, None]
    variance = jnp.mean(centered_full * centered_full, axis=-1)
    centered = lax.dynamic_slice_in_dim(
        centered_full, lax.axis_index("row") * value_rows, value_rows, 2
    )
    normed = centered * lax.rsqrt(variance + epsilon)[:, :, None] * headnorm_gain
    gated_out = (jax.nn.sigmoid(outgate_pre) * normed).astype(jnp.bfloat16)
    partial_terms = jnp.einsum("shj,hjd->sd", gated_out, w_out, preferred_element_type=jnp.float32)
    position = lax.axis_index("row") * lax.axis_size("head") + lax.axis_index("head")
    share_width = hidden.shape[1] // (lax.axis_size("row") * lax.axis_size("head"))
    vocab_here = w_vocab.shape[0]
    projection = lax.psum(partial_terms, ("row", "head"))
    new_full = (stream + projection).astype(jnp.bfloat16)
    final_feat = rms_round(new_full.astype(jnp.float32), final_gain)
    logits = jnp.einsum("sd,vd->sv", final_feat, w_vocab, preferred_element_type=jnp.float32)
    hidden_out = lax.dynamic_slice_in_dim(new_full, position * share_width, share_width, 1)
    local_ids = targets - position * vocab_here
    is_target = jnp.arange(vocab_here, dtype=jnp.int32)[None, :] == local_ids[:, None]
    target_term = jnp.sum(jnp.where(is_target, logits, 0.0), axis=-1)
    local_max = jnp.max(logits, axis=-1)
    local_sum = jnp.sum(jnp.exp(logits - local_max[:, None]), axis=-1)

    def combine(earlier, later):
        highest = jnp.maximum(earlier[0], later[0])
        joined = earlier[1] * jnp.exp(earlier[0] - highest) + later[1] * jnp.exp(later[0] - highest)
        return (highest, joined, earlier[2] + later[2])

    highest, exp_total, picked = joined_2(
        (local_max, local_sum, target_term), ("row", "head"), combine
    )
    log_prob = picked - (highest + jnp.log(exp_total))
    return (memory_out, normalizer_out, stabilizer_out, hidden_out, log_prob)


def solution(mesh):
    in_specs = (
        P("groups", None),
        P(),
        P("head", "row", None),
        P("head", "row", None),
        P("head", "row", None),
        P("head", "row", None),
        P("head", "row", None),
        P(None, "head", None),
        P(None, "head"),
        P("head", "row"),
        P(),
        P(("row", "head"), None),
        P("groups", "head", "row", None),
        P("groups", "head", "row"),
        P("groups", "head"),
        P("groups"),
    )
    out_specs = (
        P("groups", "head", "row", None),
        P("groups", "head", "row"),
        P("groups", "head"),
        P("groups", ("row", "head")),
        P("groups"),
    )
    return jax.shard_map(
        per_device, mesh=mesh, in_specs=in_specs, out_specs=out_specs, check_vma=False
    )
```

profile of v0, /device:TPU:0, one launch (start us, length us, event | category | flops | bytes accessed | tf_op | source)
XLA Modules:
  0.0 280.0 jit_solution(1592682969917463788)
XLA Ops:
  7.2 1.2 fusion.17
  8.5 2.7 convolution_convert_fusion
  11.3 33.0 %all_gather.21 = bf16[24,4,512]{0,1,2:T(4,128)(2,1)S(1)} all-gather(bf16[24,4,64]{0,1,2:T(4,128)(2,1)S(1)} %copy.34), channel_id=1, replica_groups=mesh['groups'=2,'row'=8,'head'=2] {'row'}, dimensions={2}, use_global_device_ids=true | all-gather | bytes 110592 | tf_op jit(solution)/shard_map/all_gather | solution.py:65
  44.7 1.2 fusion.13
  45.9 0.7 subtract_exponential_fusion.1
  46.7 2.2 fusion.28
  48.9 2.2 fusion.7
  51.1 3.4 %multiply_add_fusion = f32[24,4,32,512]{3,2,1,0:T(8,128)S(1)} fusion(f32[24,4,32,512]{3,2,1,0:T(8,128)} %param.30, f32[24,4,512]{2,1,0:T(4,128)S(1)} %copy.36, f32[24,4,32]{2,1,0:T(4,128)S(1)} %copy.33, f32[24,4]{1,0:T(8,128)S(1)} %copy.32), kind=kLoop, calls=%fused_computation.10 | loop fusion | flops 4718592 | bytes 12792192 | tf_op jit(solution)/shard_map/add | solution.py:63
  54.5 2.7 copy-done.1
  57.2 3.1 %fusion.26 = f32[24,4,1,512]{3,2,1,0:T(1,128)S(1)} fusion(f32[24,4,32,512]{3,2,1,0:T(8,128)S(1)} %multiply_add_fusion, f32[24,4,32,1]{2,0,1,3:T(8,128)S(1)} %fusion.7), kind=kOutput, calls=%fused_computation.46 | convolution fusion | flops 18874368 | bytes 6500352 | tf_op jit(solution)/shard_map/shj,shje->she/dot_general | solution.py:68
  60.4 0.7 copy.47
  61.2 0.6 copy.38
  61.8 0.6 dynamic-slice
  63.1 70.0 %all-reduce.7.cloned.1.call-done = f32[24,4,512]{2,0,1:T(8,128)} async-done(((f32[24,4,512]{2,0,1:T(8,128)}), f32[24,4,512]{2,0,1:T(8,128)}) %all-reduce.7.cloned.1.call-update) | async-done | bytes 196624 | tf_op jit(solution)/shard_map/psum | solution.py:71
  133.1 1.0 reduce_sum.55
  134.1 1.1 multiply_reduce_fusion
  135.3 3.8 %convolution_bitcast_fusion = f32[24,4096]{1,0:T(8,128)} fusion(bf16[4,64,4096]{2,1,0:T(8,128)(2,1)S(1)} %copy-done, bf16[4,64,4096]{2,1,0:T(8,128)(2,1)} %param.23, f32[24,4,512]{2,0,1:T(8,128)S(1)} %get-tuple-element.86, s32[]{:T(128)S(6)} %select_n.16, f32[4,64]{1,0:T(4,128)S(1)} %copy-done.6, f32[24,4]{0,1:T(4,128)S(1)} %add_rsqrt_fusion, ...), kind=kOutput, calls=%fused_computation.11 | convolution fusion | flops 101099520 | bytes 4854276 | tf_op jit(solution)/shard_map/shj,hjd->sd/dot_general | solution.py:80
  139.1 90.6 %all-reduce.9.cloned.1.call-done = f32[24,4096]{1,0:T(8,128)} async-done(((f32[24,4096]{1,0:T(8,128)}), f32[24,4096]{1,0:T(8,128)}) %all-reduce.9.cloned.1.call-update) | async-done | bytes 393232 | tf_op jit(solution)/shard_map/psum | solution.py:84
  229.6 1.2 fusion.14
  230.8 8.3 %fusion.50 = (f32[24]{0:T(128)S(1)}, f32[24,1572]{1,0:T(8,128)S(1)}) fusion(bf16[1572,4096]{1,0:T(8,128)(2,1)} %param.29, bf16[24,4096]{1,0:T(8,128)(2,1)S(1)} %get-tuple-element.84, f32[4096]{0:T(1024)S(1)} %copy-done.4, f32[24]{0:T(128)S(1)} %add_rsqrt_fusion.1), kind=kOutput, calls=%fused_computation.74 | convolution fusion | flops 309498688 | bytes 13241920 | tf_op jit(solution)/shard_map/sd,vd->sv/dot_general | solution.py:87
  240.0 30.9 %all-reduce.3 = (f32[384]{0:T(512)S(1)}, f32[384]{0:T(512)S(1)}, f32[384]{0:T(512)S(1)}) all-reduce(f32[384]{0:T(512)S(1)} %dynamic-update-slice, f32[384]{0:T(512)S(1)} %dynamic-update-slice.1, f32[384]{0:T(512)S(1)} %dynamic-update-slice.2), channel_id=2, replica_groups=mesh['groups'=2,'row'=8,'head'=2] {'row','head'}, use_global_device_ids=true, to_apply=%add | all-reduce | flops 1152 | bytes 9216
  271.2 0.6 constant_dynamic-slice_fusion.3
  272.0 0.6 while.14
  272.7 0.5 add_subtract_fusion
  (63 shorter events, 2.6 us)
Async XLA Ops:
  7.2 128.1 %copy-start = (bf16[4,64,4096]{2,1,0:T(8,128)(2,1)S(1)}, bf16[4,64,4096]{2,1,0:T(8,128)(2,1)}, u32[]{:S(2)}) copy-start(bf16[4,64,4096]{2,1,0:T(8,128)(2,1)} %param.24) | copy-start | bytes 6291460
  7.2 125.9 %all-reduce.7.cloned.1.call-start = ((), (), s32[]{:S(2)}) async-start(), calls=%async_computation | async-start | bytes 393216 | tf_op jit(solution)/shard_map/psum | solution.py:71
  46.6 7.9 %copy-start.5 = (f32[24,4]{0,1:T(4,128)}, f32[24,4]{0,1:T(4,128)S(1)}, u32[]{:S(2)}) copy-start(f32[24,4]{0,1:T(4,128)S(1)} %get-tuple-element.88) | copy-start | bytes 1156
  54.5 2.7 copy-start.1
  57.2 4.6 %copy-start.8 = (u32[32]{0:T(128)S(1)}, u32[32]{0:T(128)}, u32[]{:S(2)}) copy-start(u32[32]{0:T(128)} %constant.57) | copy-start | bytes 388
  57.2 78.0 %copy-start.2 = (bf16[24,4096]{1,0:T(8,128)(2,1)S(1)}, bf16[24,4096]{1,0:T(8,128)(2,1)}, u32[]{:S(2)}) copy-start(bf16[24,4096]{1,0:T(8,128)(2,1)} %param.18) | copy-start | bytes 589828
  57.2 78.0 %copy-start.3 = (f32[4096]{0:T(1024)S(1)}, f32[4096]{0:T(1024)}, u32[]{:S(2)}) copy-start(f32[4096]{0:T(1024)} %param.19) | copy-start | bytes 49156
  57.2 78.1 %copy-start.6 = (f32[4,64]{1,0:T(4,128)S(1)}, f32[4,64]{1,0:T(4,128)}, u32[]{:S(2)}) copy-start(f32[4,64]{1,0:T(4,128)} %param.27) | copy-start | bytes 3076
  57.2 81.8 %copy-start.7 = (s32[24]{0:T(128)S(1)}, s32[24]{0:T(128)}, u32[]{:S(2)}) copy-start(s32[24]{0:T(128)} %param.33) | copy-start | bytes 292
  57.2 173.6 %copy-start.4 = (f32[4096]{0:T(1024)S(1)}, f32[4096]{0:T(1024)}, u32[]{:S(2)}) copy-start(f32[4096]{0:T(1024)} %param.28) | copy-start | bytes 49156
  61.1 168.5 %all-reduce.9.cloned.1.call-start = ((), (), s32[]{:S(2)}) async-start(), calls=%async_computation.1 | async-start | bytes 786432 | tf_op jit(solution)/shard_map/psum | solution.py:84
Sparse Core Ops, SparseCore 0:
  61.2 71.7 all-reduce.6
  139.2 90.4 all-reduce.8
where the time goes:
time: 281 us; the launch traced here: 280 us
  waiting for transfers between devices  161 us (57%)
  blocking collectives  64 us (23%)
  matrix products  23.4 us (8%)
  between operations  15 us (5%)
  other arithmetic  9.78 us (3%)
  local copies, waits for them, and re-layouts  7.02 us (2%)
    psum x1, waiting for transfers between devices, per_device(): projection = lax.psum(partial_terms, ('row', 'head'))  90.6 us
    psum x1, waiting for transfers between devices, per_device(): readout = lax.psum(partial_readout, 'row')  70 us
    all_gather x1, blocking collectives, per_device(): lax.all_gather(value_part, 'row', axis=2, tiled=True).astype(jnp.float32)  33 us
    unnamed x1, blocking collectives  30.9 us
    dot_general x1, matrix products, per_device(): jnp.einsum('sd,vd->sv', final_feat, w_vocab, preferred_element_type=jnp.f...  8.26 us
    dot_general x3, matrix products, project(): jnp.einsum('sd,hjd->shj', normed_in, weights, preferred_element_type=jnp....  7.03 us
  transfers between devices with their start and end apart: 2, of which 2 were waited for; matrix products, arithmetic and copies ran while one was open for 0% of the time, Pallas kernels for 0%

commit v1 on v0

--- a/solution.py
+++ b/solution.py
@@ -81,7 +81,7 @@
     position = lax.axis_index("row") * lax.axis_size("head") + lax.axis_index("head")
     share_width = hidden.shape[1] // (lax.axis_size("row") * lax.axis_size("head"))
     vocab_here = w_vocab.shape[0]
-    projection = lax.psum(partial_terms, ("row", "head"))
+    projection = lax.psum(lax.psum(partial_terms, "row"), "head")
     new_full = (stream + projection).astype(jnp.bfloat16)
     final_feat = rms_round(new_full.astype(jnp.float32), final_gain)
     logits = jnp.einsum("sd,vd->sv", final_feat, w_vocab, preferred_element_type=jnp.float32)

time: 281 us -> 284 us (1.011)
  blocking collectives: 64 us -> 67.4 us
    unnamed x1, blocking collectives: 30.9 us -> 34.4 us
    psum x1 -> x2, waiting for transfers between devices: 90.6 us -> 88.9 us  [per_device(): projection = lax.psum(lax.psum(partial_terms, 'row'), 'head')]
  transfers between devices with their start and end apart: 2 -> 3, of which waited for: 2 -> 3; matrix products, arithmetic and copies ran while one was open for 0% -> 0% of each run, Pallas kernels for 0% -> 0%
where the time goes in v1:
time: 284 us; the launch traced here: 283 us
  waiting for transfers between devices  161 us (57%)
  blocking collectives  67.4 us (24%)
  matrix products  23.4 us (8%)
  between operations  14.7 us (5%)
  other arithmetic  9.78 us (3%)
  local copies, waits for them, and re-layouts  7.02 us (2%)
    psum x2, waiting for transfers between devices, per_device(): projection = lax.psum(lax.psum(partial_terms, 'row'), 'head')  88.9 us
    psum x1, waiting for transfers between devices, per_device(): readout = lax.psum(partial_readout, 'row')  71.9 us
    unnamed x1, blocking collectives  34.4 us
    all_gather x1, blocking collectives, per_device(): lax.all_gather(value_part, 'row', axis=2, tiled=True).astype(jnp.float32)  33 us
    dot_general x1, matrix products, per_device(): jnp.einsum('sd,vd->sv', final_feat, w_vocab, preferred_element_type=jnp.f...  8.26 us
    dot_general x3, matrix products, project(): jnp.einsum('sd,hjd->shj', normed_in, weights, preferred_element_type=jnp....  7.03 us
  transfers between devices with their start and end apart: 3, of which 3 were waited for; matrix products, arithmetic and copies ran while one was open for 0% of the time, Pallas kernels for 0%

profile of v1, /device:TPU:0, one launch (start us, length us, event | category | flops | bytes accessed | tf_op | source)
XLA Modules:
  0.0 283.4 jit_solution(493557090273110360)
XLA Ops:
  7.2 1.2 fusion.17
  8.5 2.7 convolution_convert_fusion
  11.3 33.0 %all_gather.21 = bf16[24,4,512]{0,1,2:T(4,128)(2,1)S(1)} all-gather(bf16[24,4,64]{0,1,2:T(4,128)(2,1)S(1)} %copy.34), channel_id=1, replica_groups=mesh['groups'=2,'row'=8,'head'=2] {'row'}, dimensions={2}, use_global_device_ids=true | all-gather | bytes 110592 | tf_op jit(solution)/shard_map/all_gather | solution.py:65
  44.7 1.2 fusion.13
  45.9 0.7 subtract_exponential_fusion.1
  46.7 2.2 fusion.28
  48.9 2.2 fusion.7
  51.1 3.4 %multiply_add_fusion = f32[24,4,32,512]{3,2,1,0:T(8,128)S(1)} fusion(f32[24,4,32,512]{3,2,1,0:T(8,128)} %param.30, f32[24,4,512]{2,1,0:T(4,128)S(1)} %copy.36, f32[24,4,32]{2,1,0:T(4,128)S(1)} %copy.33, f32[24,4]{1,0:T(8,128)S(1)} %copy.32), kind=kLoop, calls=%fused_computation.10 | loop fusion | flops 4718592 | bytes 12792192 | tf_op jit(solution)/shard_map/add | solution.py:63
  54.5 2.7 copy-done.1
  57.2 3.1 %fusion.26 = f32[24,4,1,512]{3,2,1,0:T(1,128)S(1)} fusion(f32[24,4,32,512]{3,2,1,0:T(8,128)S(1)} %multiply_add_fusion, f32[24,4,32,1]{2,0,1,3:T(8,128)S(1)} %fusion.7), kind=kOutput, calls=%fused_computation.46 | convolution fusion | flops 18874368 | bytes 6500352 | tf_op jit(solution)/shard_map/shj,shje->she/dot_general | solution.py:68
  60.4 0.7 copy.47
  61.2 71.9 %all-reduce.8.cloned.1.call-done = f32[24,4,512]{2,0,1:T(8,128)} async-done(((f32[24,4,512]{2,0,1:T(8,128)}), f32[24,4,512]{2,0,1:T(8,128)}) %all-reduce.8.cloned.1.call-update) | async-done | bytes 196624 | tf_op jit(solution)/shard_map/psum | solution.py:71
  133.1 1.0 reduce_sum.55
  134.1 1.1 multiply_reduce_fusion
  135.3 3.8 %convolution_bitcast_fusion = f32[24,4096]{1,0:T(8,128)} fusion(bf16[4,64,4096]{2,1,0:T(8,128)(2,1)S(1)} %copy-done, bf16[4,64,4096]{2,1,0:T(8,128)(2,1)} %param.23, f32[24,4,512]{2,0,1:T(8,128)S(1)} %get-tuple-element.86, s32[]{:T(128)S(6)} %select_n.16, f32[4,64]{1,0:T(4,128)S(1)} %copy-done.6, f32[24,4]{0,1:T(4,128)S(1)} %add_rsqrt_fusion, ...), kind=kOutput, calls=%fused_computation.11 | convolution fusion | flops 101099520 | bytes 4854276 | tf_op jit(solution)/shard_map/shj,hjd->sd/dot_general | solution.py:80
  139.1 71.0 %all-reduce.10.cloned.1.call-done = f32[24,4096]{1,0:T(8,128)} async-done(((f32[24,4096]{1,0:T(8,128)}), f32[24,4096]{1,0:T(8,128)}) %all-reduce.10.cloned.1.call-update) | async-done | bytes 393232 | tf_op jit(solution)/shard_map/psum | solution.py:84
  210.1 0.6 copy.38
  210.7 0.6 dynamic-slice
  212.0 17.9 %all-reduce.12.cloned.1.call-done = f32[24,4096]{1,0:T(8,128)} async-done(((f32[24,4096]{1,0:T(8,128)}), f32[24,4096]{1,0:T(8,128)}) %all-reduce.12.cloned.1.call-update) | async-done | bytes 393232 | tf_op jit(solution)/shard_map/psum | solution.py:84
  229.9 1.2 fusion.14
  231.0 8.3 %fusion.50 = (f32[24]{0:T(128)S(1)}, f32[24,1572]{1,0:T(8,128)S(1)}) fusion(bf16[1572,4096]{1,0:T(8,128)(2,1)} %param.29, bf16[24,4096]{1,0:T(8,128)(2,1)S(1)} %get-tuple-element.84, f32[4096]{0:T(1024)S(1)} %copy-done.4, f32[24]{0:T(128)S(1)} %add_rsqrt_fusion.1), kind=kOutput, calls=%fused_computation.74 | convolution fusion | flops 309498688 | bytes 13241920 | tf_op jit(solution)/shard_map/sd,vd->sv/dot_general | solution.py:87
  240.2 34.4 %all-reduce.3 = (f32[384]{0:T(512)S(1)}, f32[384]{0:T(512)S(1)}, f32[384]{0:T(512)S(1)}) all-reduce(f32[384]{0:T(512)S(1)} %dynamic-update-slice, f32[384]{0:T(512)S(1)} %dynamic-update-slice.1, f32[384]{0:T(512)S(1)} %dynamic-update-slice.2), channel_id=2, replica_groups=mesh['groups'=2,'row'=8,'head'=2] {'row','head'}, use_global_device_ids=true, to_apply=%add | all-reduce | flops 1152 | bytes 9216
  274.8 0.6 constant_dynamic-slice_fusion.3
  275.7 0.6 while.14
  (66 shorter events, 3.1 us)
Async XLA Ops:
  7.2 128.1 %copy-start = (bf16[4,64,4096]{2,1,0:T(8,128)(2,1)S(1)}, bf16[4,64,4096]{2,1,0:T(8,128)(2,1)}, u32[]{:S(2)}) copy-start(bf16[4,64,4096]{2,1,0:T(8,128)(2,1)} %param.24) | copy-start | bytes 6291460
  7.2 125.9 %all-reduce.8.cloned.1.call-start = ((), (), s32[]{:S(2)}) async-start(), calls=%async_computation | async-start | bytes 393216 | tf_op jit(solution)/shard_map/psum | solution.py:71
  46.6 7.9 %copy-start.5 = (f32[24,4]{0,1:T(4,128)}, f32[24,4]{0,1:T(4,128)S(1)}, u32[]{:S(2)}) copy-start(f32[24,4]{0,1:T(4,128)S(1)} %get-tuple-element.88) | copy-start | bytes 1156
  54.5 2.7 copy-start.1
  57.2 78.0 %copy-start.2 = (bf16[24,4096]{1,0:T(8,128)(2,1)S(1)}, bf16[24,4096]{1,0:T(8,128)(2,1)}, u32[]{:S(2)}) copy-start(bf16[24,4096]{1,0:T(8,128)(2,1)} %param.18) | copy-start | bytes 589828
  57.2 78.0 %copy-start.3 = (f32[4096]{0:T(1024)S(1)}, f32[4096]{0:T(1024)}, u32[]{:S(2)}) copy-start(f32[4096]{0:T(1024)} %param.19) | copy-start | bytes 49156
  57.2 78.1 %copy-start.6 = (f32[4,64]{1,0:T(4,128)S(1)}, f32[4,64]{1,0:T(4,128)}, u32[]{:S(2)}) copy-start(f32[4,64]{1,0:T(4,128)} %param.27) | copy-start | bytes 3076
  57.2 153.5 %copy-start.8 = (u32[32]{0:T(128)S(1)}, u32[32]{0:T(128)}, u32[]{:S(2)}) copy-start(u32[32]{0:T(128)} %constant.57) | copy-start | bytes 388
  57.2 154.7 %copy-start.7 = (s32[24]{0:T(128)S(1)}, s32[24]{0:T(128)}, u32[]{:S(2)}) copy-start(s32[24]{0:T(128)} %param.33) | copy-start | bytes 292
  57.2 173.8 %copy-start.4 = (f32[4096]{0:T(1024)S(1)}, f32[4096]{0:T(1024)}, u32[]{:S(2)}) copy-start(f32[4096]{0:T(1024)} %param.28) | copy-start | bytes 49156
  61.1 148.9 %all-reduce.10.cloned.1.call-start = ((), (), s32[]{:S(2)}) async-start(), calls=%async_computation.1 | async-start | bytes 786432 | tf_op jit(solution)/shard_map/psum | solution.py:84
  139.0 90.8 %all-reduce.12.cloned.1.call-start = ((), (), s32[]{:S(2)}) async-start(), calls=%async_computation.2 | async-start | bytes 786432 | tf_op jit(solution)/shard_map/psum | solution.py:84
Sparse Core Ops, SparseCore 0:
  61.2 71.7 all-reduce.7
  139.2 70.8 all-reduce.9
  212.4 17.4 all-reduce.11
